TPU v7x, 32 devices: a whole 2x2x4 slice. The times are simulated.
32 devices in a mesh: net: 4 (over y, x), line: 8 (over z, core).
Axes of the slice: x: 2, y: 2, z: 4, core: 2. Of those that a mesh axis runs over, the one named last changes fastest.
Arguments:
- conductance_inverse: float32 [4, 4096, 4096], P('net', 'line'), may hold values from -0.5 to 4.5, as said below
- prior_voltage: float32 [4, 96, 4096], P('net', None, 'line'), may hold values from -6 to 6
- sources: float32 [3, 4, 4096], P(None, 'net', 'line'), may hold values from -6 to 6
- fault_node: int32 [96], replicated, may hold values from 0 to 16383
- fault_conductance: float32 [96], replicated, may hold values from 0.5 to 4
- terminal_node: int32 [4, 3, 4096], P('net', None, 'line'), may hold values from 0 to 4095
- ownership: int32 [4, 4096], P('net', 'line'), may hold values from 0 to 1, as said below
- partner: int32 [4, 4096], P('net', 'line'), may hold values from 0 to 31, as said below
- delay_steps: int32 [4, 4096], P('net', 'line'), may hold values from 1 to 4, as said below
- surge_conductance: float32 [4, 4096], P('net', 'line'), may hold values from 0.2 to 1
- pole_wave: float32 [4, 6, 4096], P('net', None, 'line'), may hold values from 0.2 to 0.95
- residue_wave: float32 [4, 6, 3, 3, 4096], P('net', None, None, None, 'line'), may hold values from -1 to 1
- pole_admit: float32 [4, 6, 4096], P('net', None, 'line'), may hold values from 0.2 to 0.95
- residue_admit: float32 [4, 6, 3, 3, 4096], P('net', None, None, None, 'line'), may hold values from -1 to 1
- wave_state: float32 [4, 6, 3, 96, 4096], P('net', None, None, None, 'line'), may hold values from -4 to 4
- admit_state: float32 [4, 6, 3, 96, 4096], P('net', None, None, None, 'line'), may hold values from -4 to 4
- wave_history: float32 [4, 4, 3, 96, 4096], P('net', None, None, None, 'line'), may hold values from -6 to 6
Outputs:
- final_voltage: float32 [4, 96, 4096], P('net', None, 'line')
- end_current: float32 [4, 3, 96, 4096], P('net', None, None, 'line')
Inputs may be any that keep to these rules, and one draw needn't show every extreme that they name: `conductance_inverse`: each block is exactly symmetric. `ownership`: A slot is live exactly when the slot of the same number j % 512 at its partner owner is live; the number of live slots differs from owner to owner. The far end of slot j lies in the slot of the same number j % 512 at the partner owner, the partner of that slot is the first owner again, never the owner itself, and at most 17 live slots of one owner have the same partner; this many occur. `delay_steps`: equal at both ends of a line.
All inputs are finite; a program needn't handle non-finite values.
Results may differ from a plain program's by a relative error of at most 0.0003.
Values sent between devices are 32-bit elements; how exact they have to be, the bound alone decides.
A program may use at most 128 MiB of HBM per device.

v0:
```python
import jax
import jax.numpy as jnp
from jax import lax
from jax.sharding import PartitionSpec as P

STEPS = 3


def mix_residue(residue, vector):
    return (
        residue[:, :, 0, None, :] * vector[0]
        + residue[:, :, 1, None, :] * vector[1]
        + residue[:, :, 2, None, :] * vector[2]
    )


def select_delayed(buffer, delay_local):
    depth_count = buffer.shape[0]
    chosen = delay_local[None, :] == jnp.arange(1, depth_count + 1, dtype=jnp.int32)[:, None]
    return jnp.sum(jnp.where(chosen[:, None, None, :], buffer, 0.0), axis=0)


def terminal_values(voltage, terminal):
    picked = jnp.take(voltage, terminal.reshape(-1), axis=1)
    return jnp.moveaxis(picked.reshape(voltage.shape[0], 3, -1), 0, 1)


def spread_ends(history, terminal, node_count):
    values = jnp.moveaxis(history, 0, 1).reshape(history.shape[1], -1)
    return (
        jnp.zeros((history.shape[1], node_count), jnp.float32)
        .at[:, terminal.reshape(-1)]
        .add(values)
    )


def gather_full(block):
    return lax.all_gather(block, "line", axis=1, tiled=True)


def on_device(
    conductance_inverse,
    prior_voltage,
    sources,
    fault_node,
    fault_conductance,
    terminal_node,
    ownership,
    partner,
    delay_steps,
    surge_conductance,
    pole_wave,
    residue_wave,
    pole_admit,
    residue_admit,
    wave_state,
    admit_state,
    wave_history,
):
    inverse_block = conductance_inverse[0]
    row_count = inverse_block.shape[0]
    node_count = inverse_block.shape[1]
    line_index = lax.axis_index("line")
    net_index = lax.axis_index("net")
    offset = line_index * row_count
    net_count = lax.axis_size("net")
    line_count = lax.axis_size("line")
    devices = net_count * line_count
    slot_count = ownership.shape[1]
    capacity = (slot_count + devices - 2) // (devices - 1)
    is_live = ownership[0] > 0
    live_float = is_live.astype(jnp.float32)
    terminal = terminal_node[0]
    delay_local = delay_steps[0]
    surge_local = surge_conductance[0]
    partners = partner[0]
    slot_range = jnp.arange(slot_count, dtype=jnp.int32)
    earlier = (
        (partners[:, None] == partners[None, :])
        & is_live[None, :]
        & (slot_range[None, :] < slot_range[:, None])
    )
    slot_rank = jnp.sum(earlier.astype(jnp.int32), axis=1)
    position = jnp.where(is_live, partners * capacity + slot_rank, devices * capacity)
    scenario_range = jnp.arange(prior_voltage.shape[1], dtype=jnp.int32)
    fault_sub = fault_node // node_count
    fault_local = fault_node % node_count
    fault_here = (fault_sub == net_index) & (fault_local // row_count == line_index)
    wave_decay = pole_wave[0][:, None, None, :]
    admit_decay = pole_admit[0][:, None, None, :]
    wave_res = residue_wave[0]
    admit_res = residue_admit[0]
    voltage = gather_full(prior_voltage[0])
    voltage_rows = prior_voltage[0]
    wave_now = wave_state[0]
    admits = admit_state[0]
    history_buffer = wave_history[0]
    outgoing = None
    current = None
    for step_index in range(STEPS):
        terminal_prior = terminal_values(voltage, terminal)
        admits = admit_decay * admits + mix_residue(admit_res, terminal_prior)
        if step_index == 0:
            wave_now = wave_decay * wave_now + mix_residue(
                wave_res, select_delayed(history_buffer, delay_local)
            )
        else:
            shifted = jnp.concatenate(
                [jnp.zeros_like(history_buffer[:1]), history_buffer[:-1]], axis=0
            )
            wave_now = wave_decay * wave_now + mix_residue(
                wave_res, select_delayed(shifted, delay_local)
            )
            row_width = outgoing.shape[0] * outgoing.shape[1]
            packed = jnp.moveaxis(outgoing, 2, 0).reshape(slot_count, row_width)
            buffer = (
                jnp.zeros((devices * capacity, row_width), jnp.float32)
                .at[position]
                .set(packed, mode="drop")
            )
            arrived = lax.all_to_all(
                buffer, ("net", "line"), split_axis=0, concat_axis=0, tiled=True
            )
            picked_rows = arrived[jnp.minimum(position, devices * capacity - 1)]
            arrived = jnp.moveaxis(picked_rows.reshape(slot_count, 3, -1), 0, 2) * live_float
            newest = jnp.where((delay_local == 1)[None, None, :], arrived, 0.0)
            wave_now = wave_now + mix_residue(wave_res, newest)
            history_buffer = jnp.concatenate([arrived[None], shifted[1:]], axis=0)
        history = (jnp.sum(wave_now, axis=0) - jnp.sum(admits, axis=0)) * live_float
        injection = spread_ends(history, terminal, node_count)
        own_part = (
            lax.dynamic_slice_in_dim(injection, offset, row_count, 1)
            + sources[step_index, 0][None, :]
        )
        injection = lax.dynamic_update_slice_in_dim(injection, own_part, offset, 1)
        fault_value = voltage[scenario_range, fault_local]
        injection = injection.at[scenario_range, fault_local].add(
            jnp.where(fault_here, -fault_conductance * fault_value, 0.0)
        )
        summed = lax.psum(injection, "line")
        voltage_rows = lax.dot_general(
            summed,
            inverse_block,
            (((1,), (1,)), ((), ())),
            precision=lax.Precision.HIGHEST,
            preferred_element_type=jnp.float32,
        )
        voltage = gather_full(voltage_rows)
        terminal_now = terminal_values(voltage, terminal)
        if step_index + 1 < STEPS:
            outgoing = (2.0 * surge_local * terminal_now - history) * live_float
        else:
            current = (surge_local * terminal_now - history) * live_float
    return (voltage_rows[None], current[None])


def solution(mesh):
    return jax.shard_map(
        on_device,
        mesh=mesh,
        in_specs=(
            P("net", "line", None),
            P("net", None, "line"),
            P(None, "net", "line"),
            P(),
            P(),
            P("net", None, "line"),
            P("net", "line"),
            P("net", "line"),
            P("net", "line"),
            P("net", "line"),
            P("net", None, "line"),
            P("net", None, None, None, "line"),
            P("net", None, "line"),
            P("net", None, None, None, "line"),
            P("net", None, None, None, "line"),
            P("net", None, None, None, "line"),
            P("net", None, None, None, "line"),
        ),
        out_specs=(P("net", None, "line"), P("net", None, None, "line")),
        check_vma=False,
    )
```

profile of v0, /device:TPU:0, one launch (start us, length us, event | category | flops | bytes accessed | tf_op | source)
XLA Modules:
  0.0 577.8 jit_solution(13432879487147559588)
XLA Ops:
  32.9 8.7 %all-gather.12.cloned.1.call-done = f32[1,96,4096]{1,2,0:T(8,128)} async-done(((f32[1,96,512]{1,2,0:T(8,128)}), f32[1,96,4096]{1,2,0:T(8,128)}) %all-gather.12.cloned.1.call-update) | async-done | bytes 1572880 | tf_op jit(solution)/shard_map/all_gather | solution.py:38
  45.1 5.6 gather_fusion.5
  64.7 10.5 %scatter_custom_fusion = f32[96,4096]{0,1:T(8,128)} fusion(s32[1536]{0:T(1024)} %fusion.32, f32[1536,96]{1,0:T(8,128)} %copy.74, f32[]{:T(128)} %constant.37.clone.1), kind=kCustom, calls=%fused_computation.47 | custom fusion | flops 147456 | bytes 1573376 | tf_op jit(solution)/shard_map/scatter-add | solution.py:33
  81.1 12.2 %scatter_fusion = f32[96,4096]{1,0:T(8,128)} fusion(f32[96,4096]{1,0:T(8,128)} %copy.75, s32[96]{0:T(128)S(1)} %fusion.36, f32[96]{0:T(128)} %get-tuple-element.9), kind=kCustom, calls=%fused_computation.10 | custom fusion | flops 96 | bytes 1920 | tf_op jit(solution)/shard_map/scatter-add | solution.py:137
  93.6 61.2 %all-reduce.6.cloned.1.call-done = f32[96,4096]{1,0:T(8,128)} async-done(((f32[96,4096]{1,0:T(8,128)}), f32[96,4096]{1,0:T(8,128)}) %all-reduce.6.cloned.1.call-update) | async-done | bytes 1572880 | tf_op jit(solution)/shard_map/psum | solution.py:140
  154.8 12.7 %fusion.4 = f32[96,512]{1,0:T(8,128)} fusion(f32[96,4096]{1,0:T(8,128)} %all-reduce.6.cloned.1.call-done, f32[1,512,4096]{2,1,0:T(8,128)} %param.19), kind=kOutput, calls=%fused_computation.21 | convolution fusion | flops 2415919104 | bytes 10158080 | tf_op jit(solution)/shard_map/dot_general | solution.py:141
  174.4 17.7 %all-gather.6.cloned.1.call-done = f32[96,4096]{1,0:T(8,128)} async-done(((f32[96,512]{1,0:T(8,128)}), f32[96,4096]{1,0:T(8,128)}) %all-gather.6.cloned.1.call-update) | async-done | bytes 1572880 | tf_op jit(solution)/shard_map/all_gather | solution.py:38
  194.9 5.6 gather_fusion.6
  215.7 3.8 all-to-all-start
  234.3 4.2 fusion.11
  238.5 11.3 %all-to-all-done = f32[32,17,288]{2,1,0:T(8,128)} async-done(((f32[32,17,288]{2,1,0:T(8,128)}), f32[32,17,288]{2,1,0:T(8,128)}, u32[]{:S(2)}, u32[]{:S(2)}) %all-to-all-start) | async-done | bytes 626720 | tf_op jit(solution)/shard_map/all_to_all | solution.py:121
  256.8 3.9 fusion.38
  262.1 9.4 %scatter_custom_fusion.3 = f32[96,4096]{0,1:T(8,128)S(1)} fusion(s32[1536]{0:T(1024)} %fusion.32, f32[1536,96]{1,0:T(8,128)S(1)} %copy.84, f32[]{:T(128)} %constant.37.clone.1), kind=kCustom, calls=%fused_computation.45 | custom fusion | flops 147456 | bytes 1573376 | tf_op jit(solution)/shard_map/scatter-add | solution.py:33
  273.3 12.2 %scatter_fusion.1 = f32[96,4096]{1,0:T(8,128)} fusion(f32[96,4096]{1,0:T(8,128)} %copy.85, s32[96]{0:T(128)S(1)} %fusion.36, f32[96]{0:T(128)S(1)} %copy-done.45), kind=kCustom, calls=%fused_computation.13 | custom fusion | flops 96 | bytes 1920 | tf_op jit(solution)/shard_map/scatter-add | solution.py:137
  286.0 59.3 %all-reduce.8.cloned.1.call-done = f32[96,4096]{1,0:T(8,128)} async-done(((f32[96,4096]{1,0:T(8,128)}), f32[96,4096]{1,0:T(8,128)}) %all-reduce.8.cloned.1.call-update) | async-done | bytes 1572880 | tf_op jit(solution)/shard_map/psum | solution.py:140
  345.3 12.6 %fusion.2 = f32[96,512]{1,0:T(8,128)} fusion(f32[96,4096]{1,0:T(8,128)} %all-reduce.8.cloned.1.call-done, f32[1,512,4096]{2,1,0:T(8,128)} %param.19), kind=kOutput, calls=%fused_computation.19 | convolution fusion | flops 2415919104 | bytes 10158080 | tf_op jit(solution)/shard_map/dot_general | solution.py:141
  358.8 23.8 %all-gather.8.cloned.1.call-done = f32[96,4096]{1,0:T(8,128)} async-done(((f32[96,512]{1,0:T(8,128)}), f32[96,4096]{1,0:T(8,128)}) %all-gather.8.cloned.1.call-update) | async-done | bytes 1572880 | tf_op jit(solution)/shard_map/all_gather | solution.py:38
  412.3 4.8 add_reduce_fusion
  417.2 13.2 %all-to-all-done.1 = f32[32,17,288]{2,1,0:T(8,128)} async-done(((f32[32,17,288]{2,1,0:T(8,128)}), f32[32,17,288]{2,1,0:T(8,128)}, u32[]{:S(2)}, u32[]{:S(2)}) %all-to-all-start.1) | async-done | bytes 626720 | tf_op jit(solution)/shard_map/all_to_all | solution.py:121
  442.0 9.4 %scatter_custom_fusion.6 = f32[96,4096]{0,1:T(8,128)S(1)} fusion(s32[1536]{0:T(1024)} %fusion.32, f32[1536,96]{1,0:T(8,128)S(1)} %copy.94, f32[]{:T(128)} %constant.37.clone.1), kind=kCustom, calls=%fused_computation.43 | custom fusion | flops 147456 | bytes 1573376 | tf_op jit(solution)/shard_map/scatter-add | solution.py:33
  453.2 12.2 %scatter_fusion.2 = f32[96,4096]{1,0:T(8,128)} fusion(f32[96,4096]{1,0:T(8,128)} %copy.95, s32[96]{0:T(128)S(1)} %fusion.36, f32[96]{0:T(128)S(1)} %copy-done.44), kind=kCustom, calls=%fused_computation.16 | custom fusion | flops 96 | bytes 1920 | tf_op jit(solution)/shard_map/scatter-add | solution.py:137
  465.7 59.5 %all-reduce.10.cloned.1.call-done = f32[96,4096]{1,0:T(8,128)} async-done(((f32[96,4096]{1,0:T(8,128)}), f32[96,4096]{1,0:T(8,128)}) %all-reduce.10.cloned.1.call-update) | async-done | bytes 1572880 | tf_op jit(solution)/shard_map/psum | solution.py:140
  525.2 12.7 %fusion = f32[96,512]{1,0:T(8,128)} fusion(f32[96,4096]{1,0:T(8,128)} %all-reduce.10.cloned.1.call-done, f32[1,512,4096]{2,1,0:T(8,128)} %param.19), kind=kOutput, calls=%fused_computation.17 | convolution fusion | flops 2415919104 | bytes 10158080 | tf_op jit(solution)/shard_map/dot_general | solution.py:141
  537.9 24.6 %all-gather.10.cloned.1.call-done = f32[96,4096]{1,0:T(8,128)} async-done(((f32[96,512]{1,0:T(8,128)}), f32[96,4096]{1,0:T(8,128)}) %all-gather.10.cloned.1.call-update) | async-done | bytes 1572880 | tf_op jit(solution)/shard_map/all_gather | solution.py:38
  (215 shorter events, 151.6 us)
Async XLA Ops:
  7.2 18.5 %copy-start.46 = (s32[96]{0:T(128)S(1)}, s32[96]{0:T(128)}, u32[]{:S(2)}) copy-start(s32[96]{0:T(128)} %param.22) | copy-start | bytes 1156
  7.2 23.8 %copy-start.2 = (f32[1,6,3,96,512]{4,3,2,1,0:T(8,128)S(1)}, f32[1,6,3,96,512]{4,3,2,1,0:T(8,128)}, u32[]{:S(2)}) copy-start(f32[1,6,3,96,512]{4,3,2,1,0:T(8,128)} %param.33) | copy-start | bytes 10616836
  7.2 34.3 %all-gather.12.cloned.1.call-start = ((), (), s32[]{:S(2)}) async-start(), calls=%async_computation.8 | async-start | bytes 2359296 | tf_op jit(solution)/shard_map/all_gather | solution.py:38
  9.2 145.6 %all-reduce.6.cloned.1.call-start = ((), (), s32[]{:S(2)}) async-start(), calls=%async_computation.2 | async-start | bytes 3145728 | tf_op jit(solution)/shard_map/psum | solution.py:140
  12.5 11.2 %copy-start.35 = (s32[1536]{0:T(1024)}, s32[1536]{0:T(1024)S(1)}, u32[]{:S(2)}) copy-start(s32[1536]{0:T(1024)S(1)} %reshape_squeeze.5) | copy-start | bytes 18436
  20.2 10.8 %copy-start.25 = (f32[6,3,1,512]{3,1,2,0:T(4,128)S(1)}, f32[6,3,1,512]{3,1,2,0:T(4,128)}, u32[]{:S(2)}) copy-start(f32[6,3,1,512]{3,1,2,0:T(4,128)} %copy.124) | copy-start | bytes 110596
  20.2 10.8 %copy-start.31 = (f32[1,6,512]{2,1,0:T(8,128)S(1)}, f32[1,6,512]{2,1,0:T(8,128)}, u32[]{:S(2)}) copy-start(f32[1,6,512]{2,1,0:T(8,128)} %copy.126) | copy-start | bytes 36868
  50.7 7.7 %copy-start = (f32[1,6,3,96,512]{4,3,2,1,0:T(8,128)S(1)}, f32[1,6,3,96,512]{4,3,2,1,0:T(8,128)}, u32[]{:S(2)}) copy-start(f32[1,6,3,96,512]{4,3,2,1,0:T(8,128)} %param.34) | copy-start | bytes 10616836
  93.4 98.7 %all-gather.6.cloned.1.call-start = ((), (), s32[]{:S(2)}) async-start(), calls=%async_computation.3 | async-start | bytes 1769472 | tf_op jit(solution)/shard_map/all_gather | solution.py:38
  215.7 34.1 %all-to-all-start = ((f32[32,17,288]{2,1,0:T(8,128)}), f32[32,17,288]{2,1,0:T(8,128)}, u32[]{:S(2)}, u32[]{:S(2)}) async-start(f32[32,17,288]{2,1,0:T(8,128)} %all_to_all.16), calls=%async_computation | async-start | bytes 2359296 | tf_op jit(solution)/shard_map/all_to_all | solution.py:121
  219.5 125.8 %all-reduce.8.cloned.1.call-start = ((), (), s32[]{:S(2)}) async-start(), calls=%async_computation.4 | async-start | bytes 3145728 | tf_op jit(solution)/shard_map/psum | solution.py:140
  260.8 10.7 %copy-start.41 = (f32[1,1,512]{2,1,0:T(1,128)S(1)}, f32[1,1,512]{2,1,0:T(1,128)}, u32[]{:S(2)}) copy-start(f32[1,1,512]{2,1,0:T(1,128)} %get-tuple-element.45) | copy-start | bytes 6148
  261.8 11.6 %copy-start.45 = (f32[96]{0:T(128)S(1)}, f32[96]{0:T(128)}, u32[]{:S(2)}) copy-start(f32[96]{0:T(128)} %multiply_select_fusion.1) | copy-start | bytes 1156
  285.6 72.4 %copy-start.18 = (f32[3,96,512]{2,1,0:T(8,128)S(1)}, f32[3,96,512]{2,1,0:T(8,128)}, u32[]{:S(2)}) copy-start(f32[3,96,512]{2,1,0:T(8,128)} %get-tuple-element.3) | copy-start | bytes 1769476
  285.6 97.0 %all-gather.8.cloned.1.call-start = ((), (), s32[]{:S(2)}) async-start(), calls=%async_computation.5 | async-start | bytes 1769472 | tf_op jit(solution)/shard_map/all_gather | solution.py:38
  358.0 26.5 %copy-start.33 = (s32[2048]{0:T(1024)S(1)}, s32[2048]{0:T(1024)}, u32[]{:S(2)}) copy-start(s32[2048]{0:T(1024)} %pad_clamp_fusion) | copy-start | bytes 24580
  384.4 5.4 copy-start.11
  393.8 18.5 %copy-start.1 = (f32[1,6,3,96,512]{4,3,2,1,0:T(8,128)S(1)}, f32[1,6,3,96,512]{4,3,2,1,0:T(8,128)}, u32[]{:S(2)}) copy-start(f32[1,6,3,96,512]{4,3,2,1,0:T(8,128)} %param.34) | copy-start | bytes 10616836
  396.3 34.1 %all-to-all-start.1 = ((f32[32,17,288]{2,1,0:T(8,128)}), f32[32,17,288]{2,1,0:T(8,128)}, u32[]{:S(2)}, u32[]{:S(2)}) async-start(f32[32,17,288]{2,1,0:T(8,128)} %all_to_all.19), calls=%async_computation.1 | async-start | bytes 2359296 | tf_op jit(solution)/shard_map/all_to_all | solution.py:121
  400.1 125.1 %all-reduce.10.cloned.1.call-start = ((), (), s32[]{:S(2)}) async-start(), calls=%async_computation.6 | async-start | bytes 3145728 | tf_op jit(solution)/shard_map/psum | solution.py:140
  440.8 10.5 %copy-start.40 = (f32[1,1,512]{2,1,0:T(1,128)S(1)}, f32[1,1,512]{2,1,0:T(1,128)}, u32[]{:S(2)}) copy-start(f32[1,1,512]{2,1,0:T(1,128)} %get-tuple-element.43) | copy-start | bytes 6148
  441.7 11.5 %copy-start.44 = (f32[96]{0:T(128)S(1)}, f32[96]{0:T(128)}, u32[]{:S(2)}) copy-start(f32[96]{0:T(128)} %multiply_select_fusion) | copy-start | bytes 1156
  465.5 97.0 %all-gather.10.cloned.1.call-start = ((), (), s32[]{:S(2)}) async-start(), calls=%async_computation.7 | async-start | bytes 1769472 | tf_op jit(solution)/shard_map/all_gather | solution.py:38
  537.9 26.5 %copy-start.34 = (s32[2048]{0:T(1024)S(1)}, s32[2048]{0:T(1024)}, u32[]{:S(2)}) copy-start(s32[2048]{0:T(1024)} %pad_clamp_fusion) | copy-start | bytes 24580
  (33 other events, 88.0 us)
Sparse Core Ops, SparseCore 0:
  9.6 31.8 all-gather.11
  93.5 61.2 all-reduce.5
  167.6 24.4 all-gather.5
  285.7 59.5 all-reduce.7
  358.1 24.4 all-gather.7
  465.6 59.5 all-reduce.9
  538.0 24.4 all-gather.9
where the time goes:
time: 587 us; the launch traced here: 578 us
  waiting for transfers between devices  279 us (48%)
  other arithmetic  122 us (21%)
  local copies, waits for them, and re-layouts  115 us (20%)
  matrix products  38 us (6%)
  between operations  15.2 us (3%)
  starting transfers between devices  9.15 us (2%)
    psum x3, waiting for transfers between devices, on_device(): summed = lax.psum(injection, 'line')  180 us
    all_gather x4, waiting for transfers between devices, gather_full(): return lax.all_gather(block, 'line', axis=1, tiled=True)  74.8 us
    dot_general x3, matrix products, on_device(): lax.dot_general(summed, inverse_block, (((1,), (1,)), ((), ())), precisio...  38 us
    scatter-add x3, other arithmetic, on_device(): injection.at[scenario_range, fault_local]  36.6 us
    scatter-add x3, other arithmetic, spread_ends(): return jnp.zeros((history.shape[1], node_count), jnp.float32).at[:, termi...  29.3 us
    all_to_all x2, waiting for transfers between devices, on_device(): lax.all_to_all(buffer, ('net', 'line'), split_axis=0, concat_axis=0, tile...  24.6 us
    reduce_sum x6, other arithmetic, on_device(): history = (jnp.sum(wave_now, axis=0) - jnp.sum(admits, axis=0)) * live_float  20.3 us
    gather x4, local copies, waits for them, and re-layouts, terminal_values(): picked = jnp.take(voltage, terminal.reshape(-1), axis=1)  18.5 us
  transfers between devices with their start and end apart: 9, of which 9 were waited for; matrix products, arithmetic and copies ran while one was open for 11% of the time, Pallas kernels for 0%

commit v1 on v0

--- a/solution.py
+++ b/solution.py
@@ -35,7 +35,9 @@
 
 
 def gather_full(block):
-    return lax.all_gather(block, "line", axis=1, tiled=True)
+    return jnp.concatenate(
+        lax.all_to_all(jnp.stack([block] * lax.axis_size("line")), "line", 0, 0), axis=1
+    )
 
 
 def on_device(

time: 587 us -> 646 us (1.10)
  blocking collectives: 0 us -> 40.9 us
  starting transfers between devices: 9.15 us -> 22 us
  waiting for transfers between devices: 279 us -> 291 us
    all_to_all x0 -> x3, waiting for transfers between devices: none -> 82.1 us  [gather_full(): lax.all_to_all(jnp.stack([block] * lax.axis_size('line')), 'line', 0, 0)]
    all_gather x4 -> x0, waiting for transfers between devices: 74.8 us -> none  [gather_full(): return lax.all_gather(block, 'line', axis=1, tiled=True)]
    all_to_all x0 -> x1, blocking collectives: none -> 40.9 us  [gather_full(): lax.all_to_all(jnp.stack([block] * lax.axis_size('line')), 'line', 0, 0)]
    all_to_all x0 -> x3, starting transfers between devices: none -> 14.3 us  [gather_full(): lax.all_to_all(jnp.stack([block] * lax.axis_size('line')), 'line', 0, 0)]
    reshape x0 -> x4, local copies, waits for them, and re-layouts: none -> 8.29 us  [gather_full(): jnp.concatenate(lax.all_to_all(jnp.stack([block] * lax.axis_size('line'))...]
    unnamed x105 -> x108, local copies, waits for them, and re-layouts: 14.6 us -> 13.2 us
  transfers between devices with their start and end apart: 9 -> 8, of which waited for: 9 -> 8; matrix products, arithmetic and copies ran while one was open for 11% -> 10% of each run, Pallas kernels for 0% -> 0%
where the time goes in v1:
time: 646 us; the launch traced here: 637 us
  waiting for transfers between devices  291 us (45%)
  other arithmetic  120 us (19%)
  local copies, waits for them, and re-layouts  117 us (18%)
  blocking collectives  40.9 us (6%)
  matrix products  32.2 us (5%)
  starting transfers between devices  22 us (3%)
  between operations  15 us (2%)
    psum x3, waiting for transfers between devices, on_device(): summed = lax.psum(injection, 'line')  180 us
    all_to_all x3, waiting for transfers between devices, gather_full(): lax.all_to_all(jnp.stack([block] * lax.axis_size('line')), 'line', 0, 0)  82.1 us
    all_to_all x1, blocking collectives, gather_full(): lax.all_to_all(jnp.stack([block] * lax.axis_size('line')), 'line', 0, 0)  40.9 us
    scatter-add x3, other arithmetic, on_device(): injection.at[scenario_range, fault_local]  36.6 us
    dot_general x3, matrix products, on_device(): lax.dot_general(summed, inverse_block, (((1,), (1,)), ((), ())), precisio...  32.2 us
    scatter-add x3, other arithmetic, spread_ends(): return jnp.zeros((history.shape[1], node_count), jnp.float32).at[:, termi...  30.2 us
    all_to_all x2, waiting for transfers between devices, on_device(): lax.all_to_all(buffer, ('net', 'line'), split_axis=0, concat_axis=0, tile...  28 us
    reduce_sum x6, other arithmetic, on_device(): history = (jnp.sum(wave_now, axis=0) - jnp.sum(admits, axis=0)) * live_float  20.3 us
  transfers between devices with their start and end apart: 8, of which 8 were waited for; matrix products, arithmetic and copies ran while one was open for 10% of the time, Pallas kernels for 0%

profile of v1, /device:TPU:0, one launch (start us, length us, event | category | flops | bytes accessed | tf_op | source)
XLA Modules:
  0.0 637.2 jit_solution(6135681208076646044)
XLA Ops:
  9.5 6.4 all-to-all-start
  38.2 15.5 %all-to-all-done = f32[8,96,512]{2,1,0:T(8,128)} async-done(((f32[8,96,512]{2,1,0:T(8,128)}), f32[8,96,512]{2,1,0:T(8,128)}, u32[]{:S(2)}, u32[]{:S(2)}) %all-to-all-start) | async-done | bytes 1572896 | tf_op jit(solution)/shard_map/all_to_all | solution.py:39
  75.1 11.0 %scatter_custom_fusion = f32[96,4096]{0,1:T(8,128)} fusion(s32[1536]{0:T(1024)} %fusion.32, f32[1536,96]{1,0:T(8,128)} %copy.103, f32[]{:T(128)} %constant.37.clone.1), kind=kCustom, calls=%fused_computation.47 | custom fusion | flops 147456 | bytes 1573376 | tf_op jit(solution)/shard_map/scatter-add | solution.py:33
  91.9 12.2 %scatter_fusion = f32[96,4096]{1,0:T(8,128)} fusion(f32[96,4096]{1,0:T(8,128)} %copy.104, s32[96]{0:T(128)S(1)} %fusion.36, f32[96]{0:T(128)} %get-tuple-element.9), kind=kCustom, calls=%fused_computation.10 | custom fusion | flops 96 | bytes 1920 | tf_op jit(solution)/shard_map/scatter-add | solution.py:139
  104.2 61.0 %all-reduce.6.cloned.1.call-done = f32[96,4096]{1,0:T(8,128)} async-done(((f32[96,4096]{1,0:T(8,128)}), f32[96,4096]{1,0:T(8,128)}) %all-reduce.6.cloned.1.call-update) | async-done | bytes 1572880 | tf_op jit(solution)/shard_map/psum | solution.py:142
  165.2 10.7 %fusion.4 = f32[96,512]{1,0:T(8,128)S(1)} fusion(f32[96,4096]{1,0:T(8,128)} %all-reduce.6.cloned.1.call-done, f32[1,512,4096]{2,1,0:T(8,128)} %param.19), kind=kOutput, calls=%fused_computation.21 | convolution fusion | flops 2415919104 | bytes 10158080 | tf_op jit(solution)/shard_map/dot_general | solution.py:143
  177.3 4.3 all-to-all-start.1
  188.5 30.8 %all-to-all-done.1 = f32[8,96,512]{2,1,0:T(8,128)} async-done(((f32[8,96,512]{2,1,0:T(8,128)}), f32[8,96,512]{2,1,0:T(8,128)}, u32[]{:S(2)}, u32[]{:S(2)}) %all-to-all-start.1) | async-done | bytes 1572896 | tf_op jit(solution)/shard_map/all_to_all | solution.py:39
  222.2 5.6 gather_fusion.6
  261.2 4.2 fusion.11
  265.4 11.3 %all-to-all-done.2 = f32[32,17,288]{2,1,0:T(8,128)} async-done(((f32[32,17,288]{2,1,0:T(8,128)}), f32[32,17,288]{2,1,0:T(8,128)}, u32[]{:S(2)}, u32[]{:S(2)}) %all-to-all-start.2) | async-done | bytes 626720 | tf_op jit(solution)/shard_map/all_to_all | solution.py:123
  282.7 3.9 fusion.38
  288.0 9.8 %scatter_custom_fusion.3 = f32[96,4096]{0,1:T(8,128)S(1)} fusion(s32[1536]{0:T(1024)} %fusion.32, f32[1536,96]{1,0:T(8,128)} %copy.113, f32[]{:T(128)} %constant.37.clone.1), kind=kCustom, calls=%fused_computation.45 | custom fusion | flops 147456 | bytes 1573376 | tf_op jit(solution)/shard_map/scatter-add | solution.py:33
  299.7 12.2 %scatter_fusion.1 = f32[96,4096]{1,0:T(8,128)} fusion(f32[96,4096]{1,0:T(8,128)} %copy.114, s32[96]{0:T(128)S(1)} %fusion.36, f32[96]{0:T(128)S(1)} %copy-done.48), kind=kCustom, calls=%fused_computation.13 | custom fusion | flops 96 | bytes 1920 | tf_op jit(solution)/shard_map/scatter-add | solution.py:139
  311.9 59.7 %all-reduce.8.cloned.1.call-done = f32[96,4096]{1,0:T(8,128)} async-done(((f32[96,4096]{1,0:T(8,128)}), f32[96,4096]{1,0:T(8,128)}) %all-reduce.8.cloned.1.call-update) | async-done | bytes 1572880 | tf_op jit(solution)/shard_map/psum | solution.py:142
  371.6 10.7 %fusion.2 = f32[96,512]{1,0:T(8,128)S(1)} fusion(f32[96,4096]{1,0:T(8,128)} %all-reduce.8.cloned.1.call-done, f32[1,512,4096]{2,1,0:T(8,128)} %param.19), kind=kOutput, calls=%fused_computation.19 | convolution fusion | flops 2415919104 | bytes 10158080 | tf_op jit(solution)/shard_map/dot_general | solution.py:143
  389.4 35.8 %all-to-all-done.3 = f32[8,96,512]{2,1,0:T(8,128)S(1)} async-done(((f32[8,96,512]{2,1,0:T(8,128)}), f32[8,96,512]{2,1,0:T(8,128)S(1)}, u32[]{:S(2)}, u32[]{:S(2)}) %all-to-all-start.3) | async-done | bytes 1572896 | tf_op jit(solution)/shard_map/all_to_all | solution.py:39
  453.9 4.8 add_reduce_fusion
  458.7 16.7 %all-to-all-done.4 = f32[32,17,288]{2,1,0:T(8,128)} async-done(((f32[32,17,288]{2,1,0:T(8,128)}), f32[32,17,288]{2,1,0:T(8,128)}, u32[]{:S(2)}, u32[]{:S(2)}) %all-to-all-start.4) | async-done | bytes 626720 | tf_op jit(solution)/shard_map/all_to_all | solution.py:123
  486.9 9.4 %scatter_custom_fusion.6 = f32[96,4096]{0,1:T(8,128)S(1)} fusion(s32[1536]{0:T(1024)} %fusion.32, f32[1536,96]{1,0:T(8,128)S(1)} %copy.123, f32[]{:T(128)} %constant.37.clone.1), kind=kCustom, calls=%fused_computation.43 | custom fusion | flops 147456 | bytes 1573376 | tf_op jit(solution)/shard_map/scatter-add | solution.py:33
  498.1 12.2 %scatter_fusion.2 = f32[96,4096]{1,0:T(8,128)} fusion(f32[96,4096]{1,0:T(8,128)} %copy.124, s32[96]{0:T(128)S(1)} %fusion.36, f32[96]{0:T(128)S(1)} %copy-done.47), kind=kCustom, calls=%fused_computation.16 | custom fusion | flops 96 | bytes 1920 | tf_op jit(solution)/shard_map/scatter-add | solution.py:139
  510.3 59.7 %all-reduce.10.cloned.1.call-done = f32[96,4096]{1,0:T(8,128)} async-done(((f32[96,4096]{1,0:T(8,128)}), f32[96,4096]{1,0:T(8,128)}) %all-reduce.10.cloned.1.call-update) | async-done | bytes 1572880 | tf_op jit(solution)/shard_map/psum | solution.py:142
  570.1 10.7 %fusion = f32[96,512]{1,0:T(8,128)S(1)} fusion(f32[96,4096]{1,0:T(8,128)} %all-reduce.10.cloned.1.call-done, f32[1,512,4096]{2,1,0:T(8,128)} %param.19), kind=kOutput, calls=%fused_computation.17 | convolution fusion | flops 2415919104 | bytes 10158080 | tf_op jit(solution)/shard_map/dot_general | solution.py:143
  581.0 40.9 %all_to_all.44 = f32[8,96,512]{2,1,0:T(8,128)} all-to-all(f32[8,96,512]{2,1,0:T(8,128)S(1)} %stack.11), channel_id=1, replica_groups=mesh['net'=4,'line'=8] {'line'}, dimensions={0} | all-to-all | bytes 3145728 | tf_op jit(solution)/shard_map/all_to_all | solution.py:39
  (218 shorter events, 162.5 us)
Async XLA Ops:
  7.2 21.1 %copy-start.43 = (s32[1,512]{1,0:T(1,128)S(1)}, s32[1,512]{1,0:T(1,128)}, u32[]{:S(2)}) copy-start(s32[1,512]{1,0:T(1,128)} %param.27) | copy-start | bytes 6148
  9.5 44.3 %all-to-all-start = ((f32[8,96,512]{2,1,0:T(8,128)}), f32[8,96,512]{2,1,0:T(8,128)}, u32[]{:S(2)}, u32[]{:S(2)}) async-start(f32[8,96,512]{2,1,0:T(8,128)} %stack.8), calls=%async_computation | async-start | bytes 3145728 | tf_op jit(solution)/shard_map/all_to_all | solution.py:39
  15.8 20.5 %copy-start.2 = (f32[1,6,3,96,512]{4,3,2,1,0:T(8,128)S(1)}, f32[1,6,3,96,512]{4,3,2,1,0:T(8,128)}, u32[]{:S(2)}) copy-start(f32[1,6,3,96,512]{4,3,2,1,0:T(8,128)} %param.33) | copy-start | bytes 10616836
  15.8 149.3 %all-reduce.6.cloned.1.call-start = ((), (), s32[]{:S(2)}) async-start(), calls=%async_computation.6 | async-start | bytes 3145728 | tf_op jit(solution)/shard_map/psum | solution.py:142
  17.8 10.5 %copy-start.33 = (s32[1536]{0:T(1024)}, s32[1536]{0:T(1024)S(1)}, u32[]{:S(2)}) copy-start(s32[1536]{0:T(1024)S(1)} %reshape_squeeze.5) | copy-start | bytes 18436
  25.6 10.7 %copy-start.21 = (f32[6,3,1,512]{3,1,2,0:T(4,128)S(1)}, f32[6,3,1,512]{3,1,2,0:T(4,128)}, u32[]{:S(2)}) copy-start(f32[6,3,1,512]{3,1,2,0:T(4,128)} %copy.153) | copy-start | bytes 110596
  25.6 10.7 %copy-start.28 = (f32[1,6,512]{2,1,0:T(8,128)S(1)}, f32[1,6,512]{2,1,0:T(8,128)}, u32[]{:S(2)}) copy-start(f32[1,6,512]{2,1,0:T(8,128)} %copy.155) | copy-start | bytes 36868
  38.2 19.2 %copy-start.30 = (s32[2048]{0:T(1024)S(1)}, s32[2048]{0:T(1024)}, u32[]{:S(2)}) copy-start(s32[2048]{0:T(1024)} %pad_clamp_fusion) | copy-start | bytes 24580
  177.3 42.1 %all-to-all-start.1 = ((f32[8,96,512]{2,1,0:T(8,128)}), f32[8,96,512]{2,1,0:T(8,128)}, u32[]{:S(2)}, u32[]{:S(2)}) async-start(f32[8,96,512]{2,1,0:T(8,128)} %stack.9), calls=%async_computation.1 | async-start | bytes 3145728 | tf_op jit(solution)/shard_map/all_to_all | solution.py:39
  242.9 33.8 %all-to-all-start.2 = ((f32[32,17,288]{2,1,0:T(8,128)}), f32[32,17,288]{2,1,0:T(8,128)}, u32[]{:S(2)}, u32[]{:S(2)}) async-start(f32[32,17,288]{2,1,0:T(8,128)} %all_to_all.30), calls=%async_computation.2 | async-start | bytes 2359296 | tf_op jit(solution)/shard_map/all_to_all | solution.py:123
  246.5 125.1 %all-reduce.8.cloned.1.call-start = ((), (), s32[]{:S(2)}) async-start(), calls=%async_computation.7 | async-start | bytes 3145728 | tf_op jit(solution)/shard_map/psum | solution.py:142
  286.6 11.2 %copy-start.41 = (f32[1,1,512]{2,1,0:T(1,128)S(1)}, f32[1,1,512]{2,1,0:T(1,128)}, u32[]{:S(2)}) copy-start(f32[1,1,512]{2,1,0:T(1,128)} %get-tuple-element.45) | copy-start | bytes 6148
  286.8 12.9 %copy-start.48 = (f32[96]{0:T(128)S(1)}, f32[96]{0:T(128)}, u32[]{:S(2)}) copy-start(f32[96]{0:T(128)} %multiply_select_fusion.1) | copy-start | bytes 1156
  383.7 46.2 %copy-start.31 = (s32[2048]{0:T(1024)S(1)}, s32[2048]{0:T(1024)}, u32[]{:S(2)}) copy-start(s32[2048]{0:T(1024)} %pad_clamp_fusion) | copy-start | bytes 24580
  383.7 41.4 %all-to-all-start.3 = ((f32[8,96,512]{2,1,0:T(8,128)}), f32[8,96,512]{2,1,0:T(8,128)S(1)}, u32[]{:S(2)}, u32[]{:S(2)}) async-start(f32[8,96,512]{2,1,0:T(8,128)} %stack.10), calls=%async_computation.3 | async-start | bytes 3145728 | tf_op jit(solution)/shard_map/all_to_all | solution.py:39
  439.2 13.6 %copy-start.46 = (f32[96]{0:T(128)S(1)}, f32[96]{0:T(128)}, u32[]{:S(2)}) copy-start(f32[96]{0:T(128)} %param.23) | copy-start | bytes 1156
  439.2 14.7 %copy-start.1 = (f32[1,6,3,96,512]{4,3,2,1,0:T(8,128)S(1)}, f32[1,6,3,96,512]{4,3,2,1,0:T(8,128)}, u32[]{:S(2)}) copy-start(f32[1,6,3,96,512]{4,3,2,1,0:T(8,128)} %param.34) | copy-start | bytes 10616836
  441.6 33.8 %all-to-all-start.4 = ((f32[32,17,288]{2,1,0:T(8,128)}), f32[32,17,288]{2,1,0:T(8,128)}, u32[]{:S(2)}, u32[]{:S(2)}) async-start(f32[32,17,288]{2,1,0:T(8,128)} %all_to_all.34), calls=%async_computation.4 | async-start | bytes 2359296 | tf_op jit(solution)/shard_map/all_to_all | solution.py:123
  445.2 124.9 %all-reduce.10.cloned.1.call-start = ((), (), s32[]{:S(2)}) async-start(), calls=%async_computation.8 | async-start | bytes 3145728 | tf_op jit(solution)/shard_map/psum | solution.py:142
  453.9 22.9 %copy-start.38 = (s32[1024]{0:T(1024)S(1)}, s32[1024]{0:T(1024)}, u32[]{:S(2)}) copy-start(s32[1024]{0:T(1024)} %pad_clamp_fusion.1) | copy-start | bytes 12292
  485.8 10.5 %copy-start.40 = (f32[1,1,512]{2,1,0:T(1,128)S(1)}, f32[1,1,512]{2,1,0:T(1,128)}, u32[]{:S(2)}) copy-start(f32[1,1,512]{2,1,0:T(1,128)} %get-tuple-element.43) | copy-start | bytes 6148
  486.6 11.5 %copy-start.47 = (f32[96]{0:T(128)S(1)}, f32[96]{0:T(128)}, u32[]{:S(2)}) copy-start(f32[96]{0:T(128)} %multiply_select_fusion) | copy-start | bytes 1156
  580.8 43.0 %copy-start.27 = (f32[96,512]{1,0:T(8,128)}, f32[96,512]{1,0:T(8,128)S(1)}, u32[]{:S(2)}) copy-start(f32[96,512]{1,0:T(8,128)S(1)} %fusion) | copy-start | bytes 589828
  581.0 42.8 %copy-start.32 = (s32[2048]{0:T(1024)S(1)}, s32[2048]{0:T(1024)}, u32[]{:S(2)}) copy-start(s32[2048]{0:T(1024)} %pad_clamp_fusion) | copy-start | bytes 24580
  (34 other events, 100.7 us)
Sparse Core Ops, SparseCore 0:
  104.3 60.8 all-reduce.5
  312.0 59.5 all-reduce.7
  510.5 59.5 all-reduce.9
